TPU v7x, 32 devices: a whole 2x2x4 slice. The times are simulated.
32 devices in a mesh: scan: 2 (over y), angle: 16 (over z, x, core).
Axes of the slice: x: 2, y: 2, z: 4, core: 2. Of those that a mesh axis runs over, the one named last changes fastest.
Arguments:
- object_init: float32 [32, 2, 128, 1024], P(('scan', 'angle')), parts along dimension 0, may hold values from -3.6 to 3.6
- measured: bfloat16 [32, 15, 128, 128], P(('scan', 'angle')), parts along dimension 0
- positions: int32 [32, 15, 2], P(('scan', 'angle')), parts along dimension 0, may hold values from 0 to 896, as said below
- angle_list: int32 [32], P('scan'), parts along dimension 0, may hold values from 0 to 15, each once
- probe: float32 [4, 128, 128], P('scan'), parts along dimension 0, may hold values from -3 to 3
- radial: float32 [16, 1024, 1024], P('angle'), may hold values from -0.1875 to 0.1875
Outputs:
- slices: float32 [32, 2, 128, 1024], P(('scan', 'angle')), parts along dimension 0
- probe_out: float32 [4, 128, 128], P('scan'), parts along dimension 0
There are 2 independent parts, one for each index of `scan`. A program takes and returns all parts, laid end to end along the dimension named above; an argument that names none is the same for every part. Nothing has to cross between parts.
Inputs may be any that keep to these rules, and one draw needn't show every extreme that they name: `positions`: for each angle, patch number n = r * 15 + c has offsets (r * 64, c * 64) moved by at most 8 cells in each dimension and clipped so that the patch lies inside the 128 x 1024 projection.
All inputs are finite; a program needn't handle non-finite values.
Results may differ from a plain program's by a relative error of at most 0.0014.
The roundings to bfloat16 on the way count: a program that leaves them out, or rounds other values in their place, can miss the bound.
Values sent between devices are 32-bit elements; how exact they have to be, the bound alone decides.
A program may use at most 64 MiB of HBM per device.

v0:
```python
import math
import jax
import jax.numpy as jnp
from jax import lax
from jax.sharding import PartitionSpec as P

ITERS = 2
object_rate = 0.5
probe_rate = 1.0


def tables_exact(count, index_list):
    index = jnp.arange(count, dtype=jnp.int32)
    phase = index[:, None] * index_list[None, :] % count
    angle = phase.astype(jnp.float32) * (2.0 * math.pi / count)
    scale = 1.0 / math.sqrt(count)
    return (jnp.cos(angle) * scale, jnp.sin(angle) * scale)


def tables(count, index_list):
    cosine_part, sine_part = tables_exact(count, index_list)
    return (cosine_part.astype(jnp.bfloat16), sine_part.astype(jnp.bfloat16))


def left(table, field):
    return jnp.einsum("jk,nkl->njl", table, field, preferred_element_type=jnp.float32)


def right(field, table):
    return jnp.einsum("njk,kl->njl", field, table, preferred_element_type=jnp.float32)


def gradient_list(
    object_field, measured_intensity, scan_positions, probe_field, cosine_theta, sine_theta
):
    size = probe_field.shape[1]
    zero_index = jnp.zeros((), jnp.int32)
    pieces = jax.vmap(
        lambda row, col: lax.dynamic_slice(object_field, (zero_index, row, col), (2, size, size))
    )(scan_positions[:, 0], scan_positions[:, 1])
    piece_re, piece_im = (pieces[:, 0], pieces[:, 1])
    probe_re, probe_im = (probe_field[0], probe_field[1])
    wave_re = (probe_re * piece_re - probe_im * piece_im).astype(jnp.bfloat16)
    wave_im = (probe_re * piece_im + probe_im * piece_re).astype(jnp.bfloat16)
    half_re = (left(cosine_theta, wave_re) + left(sine_theta, wave_im)).astype(jnp.bfloat16)
    half_im = (left(cosine_theta, wave_im) - left(sine_theta, wave_re)).astype(jnp.bfloat16)
    farfield_real = right(half_re, cosine_theta) + right(half_im, sine_theta)
    farfield_imaginary = right(half_im, cosine_theta) - right(half_re, sine_theta)
    residual_error = (
        farfield_real * farfield_real
        + farfield_imaginary * farfield_imaginary
        - measured_intensity.astype(jnp.float32)
    )
    push_re = (residual_error * farfield_real).astype(jnp.bfloat16)
    push_im = (residual_error * farfield_imaginary).astype(jnp.bfloat16)
    back_re = (left(cosine_theta, push_re) - left(sine_theta, push_im)).astype(jnp.bfloat16)
    back_im = (left(cosine_theta, push_im) + left(sine_theta, push_re)).astype(jnp.bfloat16)
    grad_re = right(back_re, cosine_theta) - right(back_im, sine_theta)
    grad_im = right(back_im, cosine_theta) + right(back_re, sine_theta)
    step_re = probe_re * grad_re + probe_im * grad_im
    step_im = probe_re * grad_im - probe_im * grad_re
    steps_all = jnp.stack([step_re, step_im], 1)

    def place(index, total):
        start = (zero_index, scan_positions[index, 0], scan_positions[index, 1])
        current = lax.dynamic_slice(total, start, (2, size, size))
        return lax.dynamic_update_slice(total, current + steps_all[index], start)

    obj_grad = lax.fori_loop(0, scan_positions.shape[0], place, jnp.zeros_like(object_field))
    pg_re = jnp.sum(piece_re * grad_re + piece_im * grad_im, 0)
    pg_im = jnp.sum(piece_re * grad_im - piece_im * grad_re, 0)
    energy = jnp.sum(piece_re * piece_re + piece_im * piece_im)
    return (obj_grad, jnp.stack([pg_re, pg_im], 0), energy)


def angular(block, wave_cos, wave_sin):
    count = block.shape[0]
    flat = block.reshape(count, -1)
    exact = lax.Precision.HIGHEST
    part_cos = jnp.dot(wave_cos, flat, precision=exact, preferred_element_type=jnp.float32).reshape(
        block.shape
    )
    part_sin = jnp.dot(wave_sin, flat, precision=exact, preferred_element_type=jnp.float32).reshape(
        block.shape
    )
    harm_re = part_cos[:, 0] + part_sin[:, 1]
    harm_im = part_cos[:, 1] - part_sin[:, 0]
    return jnp.stack([harm_re, harm_im], 1)


def on_device(object_init, measured, positions, angle_list, probe, radial):
    size = probe.shape[1]
    cosine_theta, sine_theta = tables(size, jnp.arange(size, dtype=jnp.int32))
    object_field = object_init
    probe_field = probe
    for step in range(ITERS):

        def one(items):
            return gradient_list(
                items[0], items[1], items[2], probe_field, cosine_theta, sine_theta
            )

        obj_grads, probe_grads, energies = lax.map(one, (object_field, measured, positions))
        probe_total, energy_total = lax.psum((jnp.sum(probe_grads, 0), jnp.sum(energies)), "angle")
        peak = jnp.max(probe_field[0] * probe_field[0] + probe_field[1] * probe_field[1])
        object_field = object_field - object_rate / peak * obj_grads
        probe_field = probe_field - probe_rate * probe_total / (energy_total / (size * size))
    wave_cos, wave_sin = tables_exact(angle_list.shape[0], angle_list)
    gathered = lax.all_to_all(object_field, "angle", split_axis=2, concat_axis=0, tiled=True)
    harm = lax.all_to_all(
        angular(gathered, wave_cos, wave_sin), "angle", split_axis=0, concat_axis=2, tiled=True
    )
    slices = jnp.einsum(
        "kcrn,knm->kcrm",
        harm,
        radial,
        precision=lax.Precision.HIGHEST,
        preferred_element_type=jnp.float32,
    )
    return (slices, probe_field)


def solution(mesh):
    in_specs = (
        P(("scan", "angle"), None, None, None),
        P(("scan", "angle"), None, None, None),
        P(("scan", "angle"), None, None),
        P("scan"),
        P("scan", None, None),
        P("angle", None, None),
    )
    out_specs = (P(("scan", "angle"), None, None, None), P("scan", None, None))
    return jax.shard_map(
        on_device, mesh=mesh, in_specs=in_specs, out_specs=out_specs, check_vma=False
    )
```

profile of v0, /device:TPU:8, one launch (start us, length us, event | category | flops | bytes accessed | tf_op | source)
XLA Modules:
  0.0 385.9 jit_solution(10983038799125892460)
XLA Ops:
  8.0 1.5 copy.167
  9.5 2.7 gather_fusion
  12.3 3.3 fusion.297
  15.6 2.3 copy.237
  17.9 2.7 copy.238
  29.2 3.0 fusion.42
  33.6 3.0 pad_maximum_fusion
  36.9 67.4 %while.44 = (s32[]{:T(128)}, f32[2,128,1024]{1,0,2:T(2,128)S(1)}, s32[15,2]{0,1:T(2,128)S(1)}, f32[15,2,128,128]{3,2,0,1:T(8,128)}, s32[]{:T(128)}, /*index=5*/s32[]{:T(128)}, s32[]{:T(128)}) while((s32[]{:T(128)}, f32[2,128,1024]{1,0,2:T(2,128)S(1)}, s32[15,2]{0,1:T(2,128)S(1)}, f32[15,2,128,128]{3,2,0,1:T(8,128)}, s32[]{:T(128)}, ...), condition=%wide.region_2.3_spmd, body=%wide.region_1.2_spmd.sunk | while | flops 32773 | bytes 1441927 | solution.py:69
  105.5 3.9 %gather_fusion.1 = f32[15,2,128,128]{2,1,3,0:T(2,128)} fusion(f32[2,128,1024]{1,0,2:T(2,128)S(1)} %fusion.103, s32[15]{0:T(128)S(1)} %fusion.125), kind=kCustom, calls=%fused_computation.1 | custom fusion | bytes 3932340 | tf_op jit(solution)/shard_map/while/body/eval_jaxpr/vmap()/gather | solution.py:39
  109.5 5.4 %fusion.296 = (f32[15,1,128,128]{2,1,3,0:T(1,128)}, f32[15,1,128,128]{2,1,3,0:T(1,128)}) fusion(f32[15,2,128,128]{2,1,3,0:T(2,128)} %gather_fusion.1), kind=kLoop, calls=%fused_computation.344 | loop fusion | bytes 3932160 | tf_op jit(solution)/shard_map/while/body/eval_jaxpr/slice | solution.py:41
  114.9 26.1 %psum.29 = f32[]{:T(128)} all-reduce(f32[]{:T(128)} %get-tuple-element.271), channel_id=1, replica_groups=mesh['scan'=2,'angle'=16] {'angle'}, use_global_device_ids=true, to_apply=%region_7.8 | all-reduce | flops 1 | bytes 8 | tf_op jit(solution)/shard_map/psum | solution.py:104
  141.1 2.3 copy.239
  143.3 3.2 copy.240
  158.7 1.8 fusion.32
  162.3 56.3 %while.45 = (s32[]{:T(128)}, f32[2,128,1024]{1,0,2:T(2,128)S(1)}, s32[15,2]{0,1:T(2,128)S(1)}, f32[15,2,128,128]{3,2,0,1:T(8,128)}, s32[]{:T(128)}, /*index=5*/s32[]{:T(128)}, s32[]{:T(128)}) while((s32[]{:T(128)}, f32[2,128,1024]{1,0,2:T(2,128)S(1)}, s32[15,2]{0,1:T(2,128)S(1)}, f32[15,2,128,128]{3,2,0,1:T(8,128)}, s32[]{:T(128)}, ...), condition=%wide.region_10.11_spmd, body=%wide.region_9.10_spmd.sunk | while | flops 32773 | bytes 1441927 | solution.py:69
  219.1 1.7 bitcast_subtract_fusion
  220.8 2.4 copy.188
  223.3 35.7 %all_to_all.30 = f32[1,2,128,1024]{3,1,0,2:T(2,128)S(1)} all-to-all(f32[1,2,128,1024]{3,1,0,2:T(2,128)S(1)} %copy.188), channel_id=1, replica_groups=mesh['scan'=2,'angle'=16] {'angle'}, dimensions={2} | all-to-all | bytes 2097152 | tf_op jit(solution)/shard_map/all_to_all | solution.py:109
  263.6 1.6 copy.193
  265.2 4.9 %all-to-all-start.1 = ((f32[16,2,8,1024]{3,2,1,0:T(8,128)}), f32[16,2,8,1024]{3,2,1,0:T(8,128)S(1)}, u32[]{:S(2)}, u32[]{:S(2)}) async-start(f32[16,2,8,1024]{3,2,1,0:T(8,128)} %copy.193), calls=%async_computation.1 | async-start | bytes 2097152 | tf_op jit(solution)/shard_map/all_to_all | solution.py:110
  270.8 40.6 %psum.31 = f32[]{:T(128)} all-reduce(f32[]{:T(128)} %get-tuple-element.270), channel_id=1, replica_groups=mesh['scan'=2,'angle'=16] {'angle'}, use_global_device_ids=true, to_apply=%region_15.16 | all-reduce | flops 1 | bytes 8 | tf_op jit(solution)/shard_map/psum | solution.py:104
  312.0 58.5 %all-reduce.5.cloned.1.call-done = f32[2,128,128]{2,1,0:T(8,128)} async-done(((f32[2,128,128]{2,1,0:T(8,128)}), f32[2,128,128]{2,1,0:T(8,128)}) %all-reduce.5.cloned.1.call-update) | async-done | bytes 131088 | tf_op jit(solution)/shard_map/psum | solution.py:104
  370.5 1.6 divide_subtract_fusion
  372.1 6.8 %fusion.2 = f32[1,2,128,1024]{3,2,1,0:T(8,128)} fusion(f32[1,1024,1024]{2,1,0:T(8,128)} %param.15, f32[16,2,8,1024]{3,2,1,0:T(8,128)S(1)} %all-to-all-done.1), kind=kOutput, calls=%fused_computation.14 | convolution fusion | flops 3221225472 | bytes 6291456 | tf_op jit(solution)/shard_map/kcrn,knm->kcrm/dot_general | solution.py:113
  (254 shorter events, 82.6 us)
Async XLA Ops:
  7.2 140.1 %all-reduce.3.cloned.1.call-start = ((), (), s32[]{:S(2)}) async-start(), calls=%async_computation.2 | async-start | bytes 262144 | tf_op jit(solution)/shard_map/psum | solution.py:104
  15.6 5.0 %copy-start.3 = (f32[2,128,128]{2,1,0:T(8,128)S(1)}, f32[2,128,128]{2,1,0:T(8,128)}, u32[]{:S(2)}) copy-start(f32[2,128,128]{2,1,0:T(8,128)} %param.14) | copy-start | bytes 393220
  23.6 1.1 copy-start.1
  33.6 3.3 copy-start.7
  153.0 1.1 copy-start.2
  157.5 1.2 copy-start
  259.4 0.8 copy-start.6
  263.6 6.5 %copy-start.4 = (f32[128,128]{1,0:T(8,128)S(1)}, f32[128,128]{1,0:T(8,128)}, u32[]{:S(2)}) copy-start(f32[128,128]{1,0:T(8,128)} %get-tuple-element.266) | copy-start | bytes 196612
  263.6 6.5 %copy-start.5 = (f32[128,128]{1,0:T(8,128)S(1)}, f32[128,128]{1,0:T(8,128)}, u32[]{:S(2)}) copy-start(f32[128,128]{1,0:T(8,128)} %get-tuple-element.267) | copy-start | bytes 196612
  265.2 106.9 %all-to-all-start.1 = ((f32[16,2,8,1024]{3,2,1,0:T(8,128)}), f32[16,2,8,1024]{3,2,1,0:T(8,128)S(1)}, u32[]{:S(2)}, u32[]{:S(2)}) async-start(f32[16,2,8,1024]{3,2,1,0:T(8,128)} %copy.193), calls=%async_computation.1 | async-start | bytes 2097152 | tf_op jit(solution)/shard_map/all_to_all | solution.py:110
  270.0 100.4 %all-reduce.5.cloned.1.call-start = ((), (), s32[]{:S(2)}) async-start(), calls=%async_computation.3 | async-start | bytes 262144 | tf_op jit(solution)/shard_map/psum | solution.py:104
Sparse Core Ops, SparseCore 0:
  33.0 92.0 all-reduce.2
  274.9 95.5 all-reduce.4
where the time goes:
time: 393 us; the launch traced here: 386 us
  blocking collectives  102 us (26%)
  loops' own time  70.8 us (18%)
  waiting for transfers between devices  58.6 us (15%)
  local copies, waits for them, and re-layouts  58.4 us (15%)
  other arithmetic  42.5 us (11%)
  matrix products  31.1 us (8%)
  between operations  17.3 us (4%)
  starting transfers between devices  4.94 us (1%)
    another operation x2, loops' own time, gradient_list(): lax.fori_loop(0, scan_positions.shape[0], place, jnp.zeros_like(object_fi...  70.8 us
    psum x2, blocking collectives, on_device(): lax.psum((jnp.sum(probe_grads, 0), jnp.sum(energies)), 'angle')  66.7 us
    psum x2, waiting for transfers between devices, on_device(): lax.psum((jnp.sum(probe_grads, 0), jnp.sum(energies)), 'angle')  58.5 us
    all_to_all x1, blocking collectives, on_device(): lax.all_to_all(object_field, 'angle', split_axis=2, concat_axis=0, tiled=...  35.7 us
    add x30, other arithmetic, place(): return lax.dynamic_update_slice(total, current + steps_all[index], start)  27.9 us
    dynamic_slice x30, local copies, waits for them, and re-layouts, place(): start = (zero_index, scan_positions[index, 0], scan_positions[index, 1])  17.5 us
    unnamed x22, local copies, waits for them, and re-layouts  12.8 us
    dot_general x16, matrix products, right(): jnp.einsum('njk,kl->njl', field, table, preferred_element_type=jnp.float32)  12.7 us
  transfers between devices with their start and end apart: 3, of which 1 were waited for; matrix products, arithmetic and copies ran while one was open for 12% of the time, Pallas kernels for 0%

commit v1 on v0

--- a/solution.py
+++ b/solution.py
@@ -7,6 +7,13 @@
 ITERS = 2
 object_rate = 0.5
 probe_rate = 1.0
+
+
+def trade_parts(x, axis, split, join):
+    size = lax.axis_size(axis)
+    blocks = jnp.stack(jnp.split(x, size, axis=split), axis=0)
+    blocks = lax.all_to_all(blocks, axis, split_axis=0, concat_axis=0)
+    return jnp.concatenate(blocks, axis=join)
 
 
 def tables_exact(count, index_list):
@@ -106,7 +113,7 @@
         object_field = object_field - object_rate / peak * obj_grads
         probe_field = probe_field - probe_rate * probe_total / (energy_total / (size * size))
     wave_cos, wave_sin = tables_exact(angle_list.shape[0], angle_list)
-    gathered = lax.all_to_all(object_field, "angle", split_axis=2, concat_axis=0, tiled=True)
+    gathered = trade_parts(object_field, "angle", 2, 0)
     harm = lax.all_to_all(
         angular(gathered, wave_cos, wave_sin), "angle", split_axis=0, concat_axis=2, tiled=True
     )

time: 393 us -> 423 us (1.076)
  local copies, waits for them, and re-layouts: 58.4 us -> 100 us
  loops' own time: 70.8 us -> 59.9 us
    another operation x2 -> x20, local copies, waits for them, and re-layouts: 0.54 us -> 44.8 us  [the longest x18 44.3 us: trade_parts(): blocks = jnp.stack(jnp.split(x, size, axis=split), axis=0)]
    another operation x2, loops' own time: 70.8 us -> 59.9 us  [gradient_list(): lax.fori_loop(0, scan_positions.shape[0], place, jnp.zeros_like(object_fi...]
    unnamed x22 -> x56, local copies, waits for them, and re-layouts: 12.8 us -> 12.4 us
where the time goes in v1:
time: 423 us; the launch traced here: 416 us
  blocking collectives  102 us (24%)
  local copies, waits for them, and re-layouts  100 us (24%)
  loops' own time  59.9 us (14%)
  waiting for transfers between devices  58.6 us (14%)
  other arithmetic  41.6 us (10%)
  matrix products  31.1 us (7%)
  between operations  17.7 us (4%)
  starting transfers between devices  4.98 us (1%)
    psum x2, blocking collectives, on_device(): lax.psum((jnp.sum(probe_grads, 0), jnp.sum(energies)), 'angle')  66.6 us
    another operation x2, loops' own time, gradient_list(): lax.fori_loop(0, scan_positions.shape[0], place, jnp.zeros_like(object_fi...  59.9 us
    psum x2, waiting for transfers between devices, on_device(): lax.psum((jnp.sum(probe_grads, 0), jnp.sum(energies)), 'angle')  58.5 us
    another operation x18, local copies, waits for them, and re-layouts, trade_parts(): blocks = jnp.stack(jnp.split(x, size, axis=split), axis=0)  44.3 us
    all_to_all x1, blocking collectives, trade_parts(): blocks = lax.all_to_all(blocks, axis, split_axis=0, concat_axis=0)  35.7 us
    add x30, other arithmetic, place(): return lax.dynamic_update_slice(total, current + steps_all[index], start)  27.9 us
    dynamic_slice x30, local copies, waits for them, and re-layouts, place(): start = (zero_index, scan_positions[index, 0], scan_positions[index, 1])  17.5 us
    dot_general x16, matrix products, right(): jnp.einsum('njk,kl->njl', field, table, preferred_element_type=jnp.float32)  12.7 us
  transfers between devices with their start and end apart: 3, of which 1 were waited for; matrix products, arithmetic and copies ran while one was open for 12% of the time, Pallas kernels for 0%

profile of v1, /device:TPU:8, one launch (start us, length us, event | category | flops | bytes accessed | tf_op | source)
XLA Modules:
  0.0 416.2 jit_solution(13064165628303111224)
XLA Ops:
  10.4 2.7 gather_fusion
  13.2 3.3 fusion.297
  16.5 2.3 copy.200
  18.8 2.8 copy.201
  30.2 3.1 fusion.42
  34.6 3.0 pad_maximum_fusion
  37.9 56.5 %while.44 = (s32[]{:T(128)}, f32[2,128,1024]{1,0,2:T(2,128)S(1)}, s32[15,2]{0,1:T(2,128)S(1)}, f32[15,2,128,128]{3,2,0,1:T(8,128)}, s32[]{:T(128)}, /*index=5*/s32[]{:T(128)}, s32[]{:T(128)}) while((s32[]{:T(128)}, f32[2,128,1024]{1,0,2:T(2,128)S(1)}, s32[15,2]{0,1:T(2,128)S(1)}, f32[15,2,128,128]{3,2,0,1:T(8,128)}, s32[]{:T(128)}, ...), condition=%wide.region_2.3_spmd, body=%wide.region_1.2_spmd.sunk | while | flops 32773 | bytes 1441935 | solution.py:76
  95.7 4.0 gather_fusion.1
  99.6 5.4 %fusion.296 = (f32[15,1,128,128]{2,1,3,0:T(1,128)}, f32[15,1,128,128]{2,1,3,0:T(1,128)}) fusion(f32[15,2,128,128]{2,1,3,0:T(2,128)} %gather_fusion.1), kind=kLoop, calls=%fused_computation.375 | loop fusion | bytes 3932160 | tf_op jit(solution)/shard_map/while/body/eval_jaxpr/slice | solution.py:48
  105.0 26.1 %psum.29 = f32[]{:T(128)} all-reduce(f32[]{:T(128)} %get-tuple-element.263), channel_id=1, replica_groups=mesh['scan'=2,'angle'=16] {'angle'}, use_global_device_ids=true, to_apply=%region_7.8 | all-reduce | flops 1 | bytes 8 | tf_op jit(solution)/shard_map/psum | solution.py:111
  131.2 2.3 copy.202
  133.5 3.2 copy.203
  153.1 56.3 %while.45 = (s32[]{:T(128)}, f32[2,128,1024]{1,0,2:T(2,128)S(1)}, s32[15,2]{0,1:T(2,128)S(1)}, f32[15,2,128,128]{3,2,0,1:T(8,128)}, s32[]{:T(128)}, /*index=5*/s32[]{:T(128)}, s32[]{:T(128)}) while((s32[]{:T(128)}, f32[2,128,1024]{1,0,2:T(2,128)S(1)}, s32[15,2]{0,1:T(2,128)S(1)}, f32[15,2,128,128]{3,2,0,1:T(8,128)}, s32[]{:T(128)}, ...), condition=%wide.region_10.11_spmd, body=%wide.region_9.10_spmd.sunk | while | flops 32773 | bytes 1441935 | solution.py:76
  210.1 18.9 %slice_bitcast_fusion = (f32[1,1,2,8,1024]{3,2,4,1,0:T(2,128)}, f32[1,1,2,8,1024]{3,2,4,1,0:T(2,128)}, f32[1,1,2,8,1024]{3,2,4,1,0:T(2,128)}, f32[1,1,2,8,1024]{...) fusion(f32[1,2,128,1024]{2,1,3,0:T(2,128)S(1)} %bitcast_subtrac, ...), kind=kLoop, calls=%fused_computation.49 | loop fusion | bytes 2097152 | tf_op jit(solution)/shard_map/stack | solution.py:14
  234.5 2.0 copy.149
  240.5 2.0 copy.146
  242.5 2.0 copy.145
  244.5 2.0 copy.144
  246.5 2.0 copy.143
  254.8 35.7 %all_to_all.20 = f32[16,1,2,8,1024]{4,3,2,1,0:T(8,128)S(1)} all-to-all(f32[16,1,2,8,1024]{4,3,2,1,0:T(8,128)S(1)} %constant_dynamic-update-slice_fusion.2), channel_id=1, replica_groups=mesh['scan'=2,'angle'=16] {'angle'}, dimensions={0} | all-to-all | bytes 2097152 | tf_op jit(solution)/shard_map/all_to_all | solution.py:15
  295.4 4.9 %all-to-all-start.1 = ((f32[16,2,8,1024]{3,2,1,0:T(8,128)}), f32[16,2,8,1024]{3,2,1,0:T(8,128)S(1)}, u32[]{:S(2)}, u32[]{:S(2)}) async-start(f32[16,2,8,1024]{3,2,1,0:T(8,128)} %copy.156), calls=%async_computation.1 | async-start | bytes 2097152 | tf_op jit(solution)/shard_map/all_to_all | solution.py:117
  301.1 40.4 %psum.31 = f32[]{:T(128)} all-reduce(f32[]{:T(128)} %get-tuple-element.262), channel_id=1, replica_groups=mesh['scan'=2,'angle'=16] {'angle'}, use_global_device_ids=true, to_apply=%region_15.16 | all-reduce | flops 1 | bytes 8 | tf_op jit(solution)/shard_map/psum | solution.py:111
  342.2 58.5 %all-reduce.5.cloned.1.call-done = f32[2,128,128]{2,1,0:T(8,128)} async-done(((f32[2,128,128]{2,1,0:T(8,128)}), f32[2,128,128]{2,1,0:T(8,128)}) %all-reduce.5.cloned.1.call-update) | async-done | bytes 131088 | tf_op jit(solution)/shard_map/psum | solution.py:111
  402.2 6.8 %fusion.2 = f32[1,2,128,1024]{3,2,1,0:T(8,128)} fusion(f32[1,1024,1024]{2,1,0:T(8,128)} %param.15, f32[16,2,8,1024]{3,2,1,0:T(8,128)S(1)} %all-to-all-done.1), kind=kOutput, calls=%fused_computation.14 | convolution fusion | flops 3221225472 | bytes 6291456 | tf_op jit(solution)/shard_map/kcrn,knm->kcrm/dot_general | solution.py:120
  (302 shorter events, 105.1 us)
Async XLA Ops:
  7.2 130.2 %all-reduce.3.cloned.1.call-start = ((), (), s32[]{:S(2)}) async-start(), calls=%async_computation.2 | async-start | bytes 262144 | tf_op jit(solution)/shard_map/psum | solution.py:111
  24.6 1.1 copy-start.1
  30.2 3.8 copy-start.3
  34.6 3.3 copy-start.17
  143.7 1.1 copy-start.2
  148.3 1.2 copy-start
  253.5 0.9 copy-start.15
  253.6 1.0 copy-start.14
  253.6 1.0 copy-start.13
  253.6 1.0 copy-start.12
  253.6 1.0 copy-start.11
  253.6 1.1 copy-start.10
  253.6 1.1 copy-start.9
  253.6 1.1 copy-start.8
  253.6 1.1 copy-start.7
  253.6 1.1 copy-start.6
  254.5 36.0 %copy-start.16 = (s32[16]{0:T(128)S(1)}, s32[16]{0:T(128)}, u32[]{:S(2)}) copy-start(s32[16]{0:T(128)} %param.13) | copy-start | bytes 196
  293.8 6.6 %copy-start.4 = (f32[128,128]{1,0:T(8,128)S(1)}, f32[128,128]{1,0:T(8,128)}, u32[]{:S(2)}) copy-start(f32[128,128]{1,0:T(8,128)} %get-tuple-element.258) | copy-start | bytes 196612
  293.8 6.6 %copy-start.5 = (f32[128,128]{1,0:T(8,128)S(1)}, f32[128,128]{1,0:T(8,128)}, u32[]{:S(2)}) copy-start(f32[128,128]{1,0:T(8,128)} %get-tuple-element.259) | copy-start | bytes 196612
  295.4 106.8 %all-to-all-start.1 = ((f32[16,2,8,1024]{3,2,1,0:T(8,128)}), f32[16,2,8,1024]{3,2,1,0:T(8,128)S(1)}, u32[]{:S(2)}, u32[]{:S(2)}) async-start(f32[16,2,8,1024]{3,2,1,0:T(8,128)} %copy.156), calls=%async_computation.1 | async-start | bytes 2097152 | tf_op jit(solution)/shard_map/all_to_all | solution.py:117
  300.3 100.3 %all-reduce.5.cloned.1.call-start = ((), (), s32[]{:S(2)}) async-start(), calls=%async_computation.3 | async-start | bytes 262144 | tf_op jit(solution)/shard_map/psum | solution.py:111
Sparse Core Ops, SparseCore 0:
  34.0 92.0 all-reduce.2
  305.2 95.4 all-reduce.4
